TPU v7x, 256 devices: a whole 4x4x8 slice. The times are simulated.
256 devices in a mesh: row: 16 (over z, core), col: 16 (over y, x).
Axes of the slice: x: 4, y: 4, z: 8, core: 2. Of those that a mesh axis runs over, the one named last changes fastest.
Arguments:
- blocks: bfloat16 [256, 32, 256, 256], P('row', 'col'), may hold values from -0.0625 to 0.0625
- block_cols: int32 [256, 32], P('row', 'col'), may hold values from 0 to 48, as said below
- objective: float32 [196608], P(('col', 'row')), may hold values from -6 to 6
- lower_bound: float32 [196608], P(('col', 'row')), may hold values from -1 to -0.2
- upper_bound: float32 [196608], P(('col', 'row')), may hold values from 0.2 to 1
- right_side: float32 [65536], P(('row', 'col')), may hold values from -6 to 6
- primal_init: float32 [196608], P(('col', 'row')), may hold values from -0.2 to 0.2
- dual_init: float32 [65536], P(('row', 'col')), may hold values from 0 to 1
Outputs:
- primal_final: float32 [196608], P(('col', 'row'))
- dual_final: float32 [65536], P(('row', 'col'))
- step_norms: float32 [8, 2], replicated
Inputs may be any that keep to these rules, and one draw needn't show every extreme that they name: `block_cols`: entry j of a row block indexes column group j // 2; its live entries (below 48) are distinct within one row block and group, 48 marks an empty slot, and in every draw some row block has all 2 slots of some group live.
All inputs are finite; a program needn't handle non-finite values.
Results may differ from a plain program's by a relative error of at most 0.0015.
Values may be sent and summed in bfloat16 or wider, within the bound.
A program may use at most 64 MiB of HBM per device.

v0:
```python
import functools

import jax
import jax.numpy as jnp
from jax import lax
from jax.sharding import Mesh
from jax.sharding import PartitionSpec as P

ITERS = 8
ROW = ("row_0", "row_1")
COL = ("col_0", "col_1")
ROW_COL = ("row_0", "row_1", "col_0", "col_1")
COL_ROW = ("col_0", "col_1", "row_0", "row_1")


step_primal = 0.5
step_dual = 0.5


def gather_turned(arrays, axis, dims):
    turned = [jnp.moveaxis(a, dim, 0) for a, dim in zip(arrays, dims)]
    both = jnp.concatenate([t.reshape(len(t), -1) for t in turned], axis=1)
    whole, at, finished = (lax.all_gather(both, axis, axis=0, tiled=True), 0, [])
    for t, dim in zip(turned, dims):
        slab = whole[:, at : at + t[0].size].reshape(-1, *t.shape[1:])
        finished.append(jnp.moveaxis(slab, 0, dim))
        at += t[0].size
    return tuple(finished)


def over_pieces(array, axis):
    tiles = lax.all_gather(array, axis)
    return tiles.sum(axis=0)


def from_everyone(array, axis):
    count = lax.axis_size(axis)
    return lax.all_to_all(
        jnp.broadcast_to(array[None], (count, *array.shape)), axis, 0, 0, tiled=True
    )


def over_copies(array, axis):
    everything = from_everyone(array, axis)
    return jnp.sum(everything, axis=0)


def over_axes(array, axes):
    return functools.reduce(lax.psum, axes, array)


def per_device(
    blocks, block_cols, objective, lower_bound, upper_bound, right_side, primal_init, dual_init
):
    row_blocks = blocks.shape[0]
    slots = blocks.shape[1]
    width = blocks.shape[2]
    row_devices = lax.axis_size(ROW)
    col_devices = lax.axis_size(COL)
    primal_len = objective.shape[0]
    dual_len = right_side.shape[0]
    col_blocks = primal_len * row_devices // width
    primal_total = float(primal_len * row_devices * col_devices)
    dual_total = float(dual_len * row_devices * col_devices)
    flat_cols = block_cols.reshape(-1)
    chosen = flat_cols[:, None] == jnp.arange(col_blocks, dtype=jnp.int32)[None, :]
    chosen_half = chosen.astype(jnp.bfloat16)
    chosen_full = chosen.astype(jnp.float32)
    history = []
    primal_slab, objective_slab, lower_slab, upper_slab = gather_turned(
        (primal_init, objective, lower_bound, upper_bound), ROW, (0, 0, 0, 0)
    )
    dual_slab, right_slab = gather_turned((dual_init, right_side), COL, (0, 0))
    primal_offset = lax.axis_index(ROW) * primal_len
    dual_offset = lax.axis_index(COL) * dual_len
    for iteration in range(ITERS):
        dual_half = dual_slab.astype(jnp.bfloat16)
        dual_amount = dual_half.shape[0] // width
        products = jnp.einsum(
            "rsab,ra->rsb",
            blocks,
            dual_half.reshape(dual_amount, width),
            preferred_element_type=jnp.float32,
        ).reshape(dual_amount * slots, width)
        gradient = over_pieces(
            jnp.dot(
                chosen_full.T,
                products,
                precision=lax.Precision.HIGHEST,
                preferred_element_type=jnp.float32,
            ).reshape(-1),
            ROW,
        )
        primal_next = jnp.minimum(
            upper_slab,
            jnp.maximum(lower_slab, primal_slab - step_primal * (objective_slab - gradient)),
        )
        extrapolated = (2.0 * primal_next - primal_slab).astype(jnp.bfloat16)
        pick_amount = extrapolated.shape[0] // width
        picked = jnp.dot(
            chosen_half,
            extrapolated.reshape(pick_amount, width),
            preferred_element_type=jnp.float32,
        )
        shaped = picked.astype(jnp.bfloat16).reshape(row_blocks, slots, width)
        image_dual = over_copies(
            jnp.einsum("rsab,rsb->ra", blocks, shaped, preferred_element_type=jnp.float32).reshape(
                -1
            ),
            COL,
        )
        dual_next = jnp.maximum(dual_slab + step_dual * (right_slab - image_dual), 0.0)
        primal_step = lax.dynamic_slice_in_dim(
            primal_next - primal_slab, primal_offset, primal_len, 0
        )
        dual_step = lax.dynamic_slice_in_dim(dual_next - dual_slab, dual_offset, dual_len, 0)
        history.append(
            jnp.stack((jnp.sum(primal_step * primal_step), jnp.sum(dual_step * dual_step)))
        )
        primal_slab = primal_next
        dual_slab = dual_next
    primal_out = lax.dynamic_slice_in_dim(primal_slab, primal_offset, primal_len, 0)
    dual_out = lax.dynamic_slice_in_dim(dual_slab, dual_offset, dual_len, 0)
    stacked = jnp.stack(history)
    stacked = over_axes(stacked, ROW_COL)
    totals = jnp.array([primal_total, dual_total], jnp.float32)
    step_norms = jnp.sqrt(stacked / totals[None, :])
    return (primal_out, dual_out, step_norms)


def solution(mesh):
    split = Mesh(mesh.devices.reshape(8, 2, 4, 4), ("row_0", "row_1", "col_0", "col_1"))
    placed = (
        P(ROW, COL, None, None),
        P(ROW, COL),
        P(COL_ROW),
        P(COL_ROW),
        P(COL_ROW),
        P(ROW_COL),
        P(COL_ROW),
        P(ROW_COL),
    )
    return jax.shard_map(
        per_device,
        mesh=split,
        in_specs=placed,
        out_specs=(P(COL_ROW), P(ROW_COL), P()),
        check_vma=False,
    )
```

profile of v0, /device:TPU:1, one launch (start us, length us, event | category | flops | bytes accessed | tf_op | source)
XLA Modules:
  0.0 400.2 jit_solution(3310335284656649400)
XLA Ops:
  2.2 19.0 %all_gather.31 = f32[4096,2]{0,1:T(2,128)S(1)} all-gather(f32[256,2]{0,1:T(2,128)S(1)} %pad_maximum_fusion.1), channel_id=1, replica_groups=mesh['row_0'=8,'row_1'=2,'col_0'=4,'col_1'=4] {'col_0','col_1'}, dimensions={0}, use_global_device_ids=true | all-gather | bytes 34816 | tf_op jit(solution)/shard_map/all_gather | solution.py:23
  21.4 2.8 fusion.17
  24.6 28.1 %all-gather = f32[16,1,12288]{2,1,0:T(1,128)S(1)} all-gather(f32[1,1,12288]{2,1,0:T(1,128)S(1)} %reshape.329), channel_id=1, replica_groups=mesh['row_0'=8,'row_1'=2,'col_0'=4,'col_1'=4] {'row_0','row_1'}, dimensions={0}, use_global_device_ids=true | all-gather | bytes 835584 | tf_op jit(solution)/shard_map/all_gather | solution.py:32
  53.4 15.0 %all_gather.30 = f32[12288,4]{0,1:T(4,128)S(1)} all-gather(f32[768,4]{0,1:T(4,128)S(1)} %pad_maximum_fusion), channel_id=1, replica_groups=mesh['row_0'=8,'row_1'=2,'col_0'=4,'col_1'=4] {'row_0','row_1'}, dimensions={0}, use_global_device_ids=true | all-gather | bytes 208896 | tf_op jit(solution)/shard_map/all_gather | solution.py:23
  69.3 3.4 fusion.63
  73.6 4.7 %all-to-all-start = ((f32[16,1,4096]{2,1,0:T(1,128)}), f32[16,1,4096]{2,1,0:T(1,128)S(1)}, u32[]{:S(2)}, u32[]{:S(2)}) async-start(f32[16,1,4096]{2,1,0:T(1,128)} %broadcast_in_dim.59), calls=%async_computation | async-start | bytes 524288 | tf_op jit(solution)/shard_map/all_to_all | solution.py:38
  78.3 8.3 %all-to-all-done = f32[16,1,4096]{2,1,0:T(1,128)S(1)} async-done(((f32[16,1,4096]{2,1,0:T(1,128)}), f32[16,1,4096]{2,1,0:T(1,128)S(1)}, u32[]{:S(2)}, u32[]{:S(2)}) %all-to-all-start) | async-done | bytes 262176 | tf_op jit(solution)/shard_map/all_to_all | solution.py:38
  86.8 2.8 fusion.15
  90.1 19.1 %all-gather.1 = f32[16,1,12288]{2,1,0:T(1,128)S(1)} all-gather(f32[1,1,12288]{2,1,0:T(1,128)S(1)} %reshape.331), channel_id=1, replica_groups=mesh['row_0'=8,'row_1'=2,'col_0'=4,'col_1'=4] {'row_0','row_1'}, dimensions={0}, use_global_device_ids=true | all-gather | bytes 835584 | tf_op jit(solution)/shard_map/all_gather | solution.py:32
  109.9 3.4 fusion.64
  113.5 11.0 %all_to_all.48 = f32[16,1,4096]{2,1,0:T(1,128)S(1)} all-to-all(f32[16,1,4096]{2,1,0:T(1,128)S(1)} %broadcast_in_dim.61), channel_id=1, replica_groups=mesh['row_0'=8,'row_1'=2,'col_0'=4,'col_1'=4] {'col_0','col_1'}, dimensions={0} | all-to-all | bytes 524288 | tf_op jit(solution)/shard_map/all_to_all | solution.py:38
  124.7 2.8 fusion.13
  127.9 17.8 %all-gather.2 = f32[16,1,12288]{2,1,0:T(1,128)S(1)} all-gather(f32[1,1,12288]{2,1,0:T(1,128)S(1)} %reshape.333), channel_id=1, replica_groups=mesh['row_0'=8,'row_1'=2,'col_0'=4,'col_1'=4] {'row_0','row_1'}, dimensions={0}, use_global_device_ids=true | all-gather | bytes 835584 | tf_op jit(solution)/shard_map/all_gather | solution.py:32
  146.5 3.4 fusion.65
  150.1 11.0 %all_to_all.49 = f32[16,1,4096]{2,1,0:T(1,128)S(1)} all-to-all(f32[16,1,4096]{2,1,0:T(1,128)S(1)} %broadcast_in_dim.63), channel_id=1, replica_groups=mesh['row_0'=8,'row_1'=2,'col_0'=4,'col_1'=4] {'col_0','col_1'}, dimensions={0} | all-to-all | bytes 524288 | tf_op jit(solution)/shard_map/all_to_all | solution.py:38
  161.2 2.8 fusion.11
  164.5 19.1 %all-gather.3 = f32[16,1,12288]{2,1,0:T(1,128)S(1)} all-gather(f32[1,1,12288]{2,1,0:T(1,128)S(1)} %reshape.335), channel_id=1, replica_groups=mesh['row_0'=8,'row_1'=2,'col_0'=4,'col_1'=4] {'row_0','row_1'}, dimensions={0}, use_global_device_ids=true | all-gather | bytes 835584 | tf_op jit(solution)/shard_map/all_gather | solution.py:32
  184.3 3.4 fusion.66
  188.6 3.7 all-to-all-start.3
  192.4 8.3 %all-to-all-done.3 = f32[16,1,4096]{2,1,0:T(1,128)S(1)} async-done(((f32[16,1,4096]{2,1,0:T(1,128)}), f32[16,1,4096]{2,1,0:T(1,128)S(1)}, u32[]{:S(2)}, u32[]{:S(2)}) %all-to-all-start.3) | async-done | bytes 262176 | tf_op jit(solution)/shard_map/all_to_all | solution.py:38
  200.9 2.8 fusion.9
  204.1 17.6 %all-gather.4 = f32[16,1,12288]{2,1,0:T(1,128)S(1)} all-gather(f32[1,1,12288]{2,1,0:T(1,128)S(1)} %reshape.337), channel_id=1, replica_groups=mesh['row_0'=8,'row_1'=2,'col_0'=4,'col_1'=4] {'row_0','row_1'}, dimensions={0}, use_global_device_ids=true | all-gather | bytes 835584 | tf_op jit(solution)/shard_map/all_gather | solution.py:32
  222.4 3.4 fusion.67
  226.7 3.5 all-to-all-start.4
  230.3 8.4 %all-to-all-done.4 = f32[16,1,4096]{2,1,0:T(1,128)S(1)} async-done(((f32[16,1,4096]{2,1,0:T(1,128)}), f32[16,1,4096]{2,1,0:T(1,128)S(1)}, u32[]{:S(2)}, u32[]{:S(2)}) %all-to-all-start.4) | async-done | bytes 262176 | tf_op jit(solution)/shard_map/all_to_all | solution.py:38
  239.0 2.8 fusion.7
  242.2 18.9 %all-gather.5 = f32[16,1,12288]{2,1,0:T(1,128)S(1)} all-gather(f32[1,1,12288]{2,1,0:T(1,128)S(1)} %reshape.339), channel_id=1, replica_groups=mesh['row_0'=8,'row_1'=2,'col_0'=4,'col_1'=4] {'row_0','row_1'}, dimensions={0}, use_global_device_ids=true | all-gather | bytes 835584 | tf_op jit(solution)/shard_map/all_gather | solution.py:32
  261.9 3.4 fusion.68
  266.2 3.5 all-to-all-start.5
  269.8 8.4 %all-to-all-done.5 = f32[16,1,4096]{2,1,0:T(1,128)S(1)} async-done(((f32[16,1,4096]{2,1,0:T(1,128)}), f32[16,1,4096]{2,1,0:T(1,128)S(1)}, u32[]{:S(2)}, u32[]{:S(2)}) %all-to-all-start.5) | async-done | bytes 262176 | tf_op jit(solution)/shard_map/all_to_all | solution.py:38
  278.4 2.8 fusion.5
  281.7 17.6 %all-gather.6 = f32[16,1,12288]{2,1,0:T(1,128)S(1)} all-gather(f32[1,1,12288]{2,1,0:T(1,128)S(1)} %reshape.341), channel_id=1, replica_groups=mesh['row_0'=8,'row_1'=2,'col_0'=4,'col_1'=4] {'row_0','row_1'}, dimensions={0}, use_global_device_ids=true | all-gather | bytes 835584 | tf_op jit(solution)/shard_map/all_gather | solution.py:32
  300.0 3.4 fusion.69
  304.3 3.5 all-to-all-start.6
  307.9 8.4 %all-to-all-done.6 = f32[16,1,4096]{2,1,0:T(1,128)S(1)} async-done(((f32[16,1,4096]{2,1,0:T(1,128)}), f32[16,1,4096]{2,1,0:T(1,128)S(1)}, u32[]{:S(2)}, u32[]{:S(2)}) %all-to-all-start.6) | async-done | bytes 262176 | tf_op jit(solution)/shard_map/all_to_all | solution.py:38
  316.5 2.8 fusion.3
  319.8 18.9 %all-gather.7 = f32[16,1,12288]{2,1,0:T(1,128)S(1)} all-gather(f32[1,1,12288]{2,1,0:T(1,128)S(1)} %reshape.343), channel_id=1, replica_groups=mesh['row_0'=8,'row_1'=2,'col_0'=4,'col_1'=4] {'row_0','row_1'}, dimensions={0}, use_global_device_ids=true | all-gather | bytes 835584 | tf_op jit(solution)/shard_map/all_gather | solution.py:32
  339.4 3.4 fusion.70
  343.7 3.5 all-to-all-start.7
  348.7 7.1 %all-to-all-done.7 = f32[16,1,4096]{2,1,0:T(1,128)S(1)} async-done(((f32[16,1,4096]{2,1,0:T(1,128)}), f32[16,1,4096]{2,1,0:T(1,128)S(1)}, u32[]{:S(2)}, u32[]{:S(2)}) %all-to-all-start.7) | async-done | bytes 262176 | tf_op jit(solution)/shard_map/all_to_all | solution.py:38
  357.3 1.4 maximum_bitcast_fusion.7
  361.5 1.4 maximum_bitcast_fusion.4
  363.0 1.4 maximum_bitcast_fusion.3
  367.2 1.4 maximum_bitcast_fusion
  368.8 10.7 %psum.28 = f32[8,2]{0,1:T(2,128)S(1)} all-reduce(f32[8,2]{0,1:T(2,128)S(1)} %stack.131), channel_id=1, replica_groups=mesh['row_0'=8,'row_1'=2,'col_0'=4,'col_1'=4] {'row_0'}, use_global_device_ids=true, to_apply=%region_32.0 | all-reduce | flops 16 | bytes 128 | tf_op jit(solution)/shard_map/psum | solution.py:49
  379.5 7.0 %psum.29 = f32[8,2]{0,1:T(2,128)S(1)} all-reduce(f32[8,2]{0,1:T(2,128)S(1)} %psum.28), channel_id=1, replica_groups=mesh['row_0'=8,'row_1'=2,'col_0'=4,'col_1'=4] {'row_1'}, use_global_device_ids=true, to_apply=%region_33.0 | all-reduce | flops 16 | bytes 128 | tf_op jit(solution)/shard_map/psum | solution.py:49
  386.5 6.5 %psum.30 = f32[8,2]{0,1:T(2,128)S(1)} all-reduce(f32[8,2]{0,1:T(2,128)S(1)} %psum.29), channel_id=1, replica_groups=mesh['row_0'=8,'row_1'=2,'col_0'=4,'col_1'=4] {'col_0'}, use_global_device_ids=true, to_apply=%region_34.0 | all-reduce | flops 16 | bytes 128 | tf_op jit(solution)/shard_map/psum | solution.py:49
  393.0 6.6 %psum.31 = f32[8,2]{0,1:T(2,128)S(1)} all-reduce(f32[8,2]{0,1:T(2,128)S(1)} %psum.30), channel_id=1, replica_groups=mesh['row_0'=8,'row_1'=2,'col_0'=4,'col_1'=4] {'col_1'}, use_global_device_ids=true, to_apply=%region_35.0 | all-reduce | flops 16 | bytes 128 | tf_op jit(solution)/shard_map/psum | solution.py:49
  (159 shorter events, 28.3 us)
Async XLA Ops:
  0.6 52.7 %copy-start = (f32[768]{0:T(1024)S(1)}, f32[768]{0:T(1024)}, u32[]{:S(2)}) copy-start(f32[768]{0:T(1024)} %param.15) | copy-start | bytes 9220
  0.6 52.7 %copy-start.1 = (f32[768]{0:T(1024)S(1)}, f32[768]{0:T(1024)}, u32[]{:S(2)}) copy-start(f32[768]{0:T(1024)} %param.11) | copy-start | bytes 9220
  0.7 52.7 %copy-start.2 = (f32[768]{0:T(1024)S(1)}, f32[768]{0:T(1024)}, u32[]{:S(2)}) copy-start(f32[768]{0:T(1024)} %param.12) | copy-start | bytes 9220
  0.7 52.7 %copy-start.3 = (f32[768]{0:T(1024)S(1)}, f32[768]{0:T(1024)}, u32[]{:S(2)}) copy-start(f32[768]{0:T(1024)} %param.13) | copy-start | bytes 9220
  73.6 13.0 %all-to-all-start = ((f32[16,1,4096]{2,1,0:T(1,128)}), f32[16,1,4096]{2,1,0:T(1,128)S(1)}, u32[]{:S(2)}, u32[]{:S(2)}) async-start(f32[16,1,4096]{2,1,0:T(1,128)} %broadcast_in_dim.59), calls=%async_computation | async-start | bytes 524288 | tf_op jit(solution)/shard_map/all_to_all | solution.py:38
  188.6 12.0 %all-to-all-start.3 = ((f32[16,1,4096]{2,1,0:T(1,128)}), f32[16,1,4096]{2,1,0:T(1,128)S(1)}, u32[]{:S(2)}, u32[]{:S(2)}) async-start(f32[16,1,4096]{2,1,0:T(1,128)} %broadcast_in_dim.65), calls=%async_computation.3 | async-start | bytes 524288 | tf_op jit(solution)/shard_map/all_to_all | solution.py:38
  226.7 12.0 %all-to-all-start.4 = ((f32[16,1,4096]{2,1,0:T(1,128)}), f32[16,1,4096]{2,1,0:T(1,128)S(1)}, u32[]{:S(2)}, u32[]{:S(2)}) async-start(f32[16,1,4096]{2,1,0:T(1,128)} %broadcast_in_dim.67), calls=%async_computation.4 | async-start | bytes 524288 | tf_op jit(solution)/shard_map/all_to_all | solution.py:38
  266.2 12.0 %all-to-all-start.5 = ((f32[16,1,4096]{2,1,0:T(1,128)}), f32[16,1,4096]{2,1,0:T(1,128)S(1)}, u32[]{:S(2)}, u32[]{:S(2)}) async-start(f32[16,1,4096]{2,1,0:T(1,128)} %broadcast_in_dim.69), calls=%async_computation.5 | async-start | bytes 524288 | tf_op jit(solution)/shard_map/all_to_all | solution.py:38
  304.3 12.0 %all-to-all-start.6 = ((f32[16,1,4096]{2,1,0:T(1,128)}), f32[16,1,4096]{2,1,0:T(1,128)S(1)}, u32[]{:S(2)}, u32[]{:S(2)}) async-start(f32[16,1,4096]{2,1,0:T(1,128)} %broadcast_in_dim.71), calls=%async_computation.6 | async-start | bytes 524288 | tf_op jit(solution)/shard_map/all_to_all | solution.py:38
  319.8 79.8 %copy-start.4 = (f32[2]{0:T(128)S(1)}, f32[2]{0:T(128)}, u32[]{:S(2)}) copy-start(f32[2]{0:T(128)} %constant.46) | copy-start | bytes 28
  343.7 12.0 %all-to-all-start.7 = ((f32[16,1,4096]{2,1,0:T(1,128)}), f32[16,1,4096]{2,1,0:T(1,128)S(1)}, u32[]{:S(2)}, u32[]{:S(2)}) async-start(f32[16,1,4096]{2,1,0:T(1,128)} %broadcast_in_dim.73), calls=%async_computation.7 | async-start | bytes 524288 | tf_op jit(solution)/shard_map/all_to_all | solution.py:38
where the time goes:
time: 405 us; the launch traced here: 400 us
  blocking collectives  244 us (60%)
  matrix products  53.5 us (13%)
  waiting for transfers between devices  49 us (12%)
  starting transfers between devices  22.5 us (6%)
  other arithmetic  20.5 us (5%)
  local copies, waits for them, and re-layouts  9.56 us (2%)
    all_gather x8, blocking collectives, over_pieces(): tiles = lax.all_gather(array, axis)  157 us
    all_to_all x6, waiting for transfers between devices, from_everyone(): lax.all_to_all(jnp.broadcast_to(array[None], (count, *array.shape)), axis...  49 us
    all_gather x2, blocking collectives, gather_turned(): lax.all_gather(both, axis, axis=0, tiled=True)  34 us
    psum x4, blocking collectives, over_axes(): return functools.reduce(lax.psum, axes, array)  30.8 us
    dot_general x8, matrix products, per_device(): jnp.einsum('rsab,rsb->ra', blocks, shaped, preferred_element_type=jnp.flo...  26.9 us
    dot_general x8, matrix products, per_device(): jnp.einsum('rsab,ra->rsb', blocks, dual_half.reshape(dual_amount, width),...  22.7 us
    all_to_all x6, starting transfers between devices, from_everyone(): lax.all_to_all(jnp.broadcast_to(array[None], (count, *array.shape)), axis...  22.5 us
    all_to_all x2, blocking collectives, from_everyone(): lax.all_to_all(jnp.broadcast_to(array[None], (count, *array.shape)), axis...  21.9 us
  transfers between devices with their start and end apart: 6, of which 6 were waited for; matrix products, arithmetic and copies ran while one was open for 0% of the time, Pallas kernels for 0%

commit v1 on v0

v1 whole, which is shorter than its diff:
```python
import functools

import jax
import jax.numpy as jnp
from jax import lax
from jax.experimental import pallas as pl
from jax.experimental.pallas import tpu as pltpu
from jax.sharding import PartitionSpec as P

MESH = pl.DeviceIdType.MESH
ITERS = 8
W = 256
H = 128
NX = 4
STEP = 0.5
CHUNKS = 4
F32 = jnp.float32
BF16 = jnp.bfloat16


def hops(d, n):
    return min(d, n - d)


def ring_order(n):
    return sorted(range(1, n), key=lambda d: -hops(d, n))


def plane_order(ny, nx):
    pairs = [(dy, dx) for dy in range(ny) for dx in range(nx) if (dy, dx) != (0, 0)]
    return sorted(pairs, key=lambda p: -(hops(p[0], ny) + hops(p[1], nx)))


def kernel(
    nz, ny, nx,
    cols, blocks, objective, lower, upper, right_side, primal_init, dual_init,
    primal_out, dual_out, norms_out,
    bl, bt, mask, left, left2, slab, dslab, yf,
    pinit, pgot, dinit, dgot,
    gsend, grecv, zsend, zrecv, esend, erecv, xg, gath, xsend, xrecv,
    pacc, dacc, prow, precv, frow, frecv, plast, pstage, dstage,
    sem_blk, sem_in, sem_out,
    s_pinit, r_pinit, s_dinit, r_dinit,
    s_g, r_g, s_e, r_e, s_z, r_z, s_x, r_x,
    s_p, r_p, s_f, r_f, s_l, r_l,
):
    nrow, ncol = nz * 2, ny * nx
    rb, cb = ncol, 3 * nrow
    kg = rb * 2 * W
    row = lax.axis_index("row")
    col = lax.axis_index("col")
    z, c = row // 2, row % 2
    y, x = col // nx, col % nx
    other = 1 - c
    partner = (z * 2 + other, col)

    zpeers = [lax.rem(z + d, nz) for d in ring_order(nz)]
    xpeers = [lax.rem(y + dy, ny) * nx + lax.rem(x + dx, nx) for dy, dx in plane_order(ny, nx)]

    def remote(src, dst, ssem, rsem, dev):
        return pltpu.make_async_remote_copy(
            src_ref=src, dst_ref=dst, send_sem=ssem, recv_sem=rsem,
            device_id=dev, device_id_type=MESH,
        )

    rows_per = kg // CHUNKS
    for j in range(CHUNKS):
        pltpu.make_async_copy(
            blocks.at[pl.ds(j * rows_per, rows_per)], bl.at[pl.ds(j * rows_per, rows_per)], sem_blk.at[j]
        ).start()
    loads = []
    for q, ref in enumerate((dual_init, right_side)):
        for h in range(2):
            loads.append(pltpu.make_async_copy(ref.at[pl.ds(h * H, H)], dinit.at[q * 2 + h, 0], sem_in.at[len(loads)]))
    nd = len(loads)
    for q, ref in enumerate((primal_init, objective, lower, upper)):
        for i in range(3):
            for h in range(2):
                loads.append(
                    pltpu.make_async_copy(
                        ref.at[pl.ds(i * W + h * H, H)], pinit.at[h * 12 + q * 3 + i, 0], sem_in.at[len(loads)]
                    )
                )
    for cp in loads:
        cp.start()

    barrier = pltpu.get_barrier_semaphore()
    group = [partner]
    for zp in zpeers:
        group += [(zp * 2, col), (zp * 2 + 1, col)]
    xgroup = [(row, xp) for xp in xpeers]
    for dev in xgroup + group:
        pl.semaphore_signal(barrier, inc=1, device_id=dev, device_id_type=MESH)
    for cp in loads:
        cp.wait()
    pl.semaphore_wait(barrier, len(group) + len(xgroup))

    for i, dev in enumerate(xgroup):
        remote(dinit, dgot.at[pl.ds(col * 4, 4)], s_dinit.at[i], r_dinit.at[col], dev).start()
    pdest = [(partner, other)]
    for zp in zpeers:
        pdest += [((zp * 2 + h, col), h) for h in (0, 1)]
    for i, (dev, h) in enumerate(pdest):
        remote(pinit.at[pl.ds(h * 12, 12)], pgot.at[pl.ds(row * 12, 12)], s_pinit.at[i], r_pinit.at[row], dev).start()
    dgot[pl.ds(col * 4, 4)] = dinit[...]
    pgot[pl.ds(row * 12, 12)] = pinit[pl.ds(c * 12, 12)]

    slot_id = lax.broadcasted_iota(jnp.int32, (cb, H), 0)
    for r in range(rb):
        for s in range(2):
            mask[r * 2 + s] = jnp.where(slot_id == cols[r, s], 1.0, 0.0).astype(BF16)
    xg[...] = jnp.zeros_like(xg)
    pacc[...] = jnp.zeros_like(pacc)
    dacc[...] = jnp.zeros_like(dacc)
    eye = jnp.where(
        lax.broadcasted_iota(jnp.int32, (W, W), 0) == lax.broadcasted_iota(jnp.int32, (W, W), 1), 1.0, 0.0
    ).astype(BF16)
    for j in range(CHUNKS):
        pltpu.make_async_copy(
            blocks.at[pl.ds(j * rows_per, rows_per)], bl.at[pl.ds(j * rows_per, rows_per)], sem_blk.at[j]
        ).wait()

    def turn(rs, carry):
        block = bl[pl.ds(pl.multiple_of(rs * W, W), W), :]
        turned = lax.dot_general(eye, block, (((1,), (1,)), ((), ())), preferred_element_type=F32).astype(BF16)
        at = pl.ds(pl.multiple_of(rs * H, H), H)
        bt[0, at, :] = turned[:H]
        bt[1, at, :] = turned[H:]
        return carry

    lax.fori_loop(0, rb * 2, turn, 0)

    for i, dev in enumerate(xgroup):
        src = xpeers[i]
        remote(dinit, dgot.at[pl.ds(src * 4, 4)], s_dinit.at[i], r_dinit.at[src], dev).wait_recv()
    for g in range(ncol):
        for q in range(2):
            for h in range(2):
                dslab[q, g : g + 1, h * H : (h + 1) * H] = dgot[g * 4 + q * 2 + h]

    lane8 = lax.broadcasted_iota(jnp.int32, (8, H), 1)
    sub8 = lax.broadcasted_iota(jnp.int32, (8, H), 0)

    def to_lanes(acc, off):
        total = jnp.sum(acc, axis=1, keepdims=True)
        return jnp.sum(jnp.where(lane8 == sub8 + off, total, 0.0), axis=0, keepdims=True)

    row_id = lax.broadcasted_iota(jnp.int32, (rb, H), 0)

    def half_gradient(h):
        acc = jnp.zeros((cb, H), F32)
        lanes = pl.ds(pl.multiple_of(h * H, H), H)
        step = kg // CHUNKS
        for j in range(CHUNKS):
            acc = acc + jnp.dot(
                left[:, j * step : (j + 1) * step], bl[j * step : (j + 1) * step, lanes], preferred_element_type=F32
            )
        return acc

    def half_image(which, h):
        for r in range(rb):
            for s in range(2):
                gath[s, r : r + 1, :] = xg[which, pl.ds(cols[r, s], 1), :]
        picked = [gath[s].astype(BF16) for s in range(2)]
        for r in range(rb):
            keep = jnp.where(row_id == r, 1.0, 0.0).astype(BF16)
            for s in range(2):
                left2[:, (r * 2 + s) * H : (r * 2 + s + 1) * H] = picked[s] * keep
        acc = jnp.zeros((rb, W), F32)
        step = rb * W // CHUNKS
        for j in range(CHUNKS):
            acc = acc + jnp.dot(
                left2[:, j * step : (j + 1) * step], bt[h, j * step : (j + 1) * step, :], preferred_element_type=F32
            )
        return acc

    def iteration(k, carry):
        par = lax.rem(k, 2)
        yf[...] = dslab[0].astype(BF16).astype(F32)
        for r in range(rb):
            wide = jnp.broadcast_to(yf[r : r + 1, :], (cb, W)).astype(BF16)
            for s in range(2):
                m = mask[r * 2 + s]
                for h in range(2):
                    at = (r * 2 + s) * W + h * H
                    left[:, at : at + H] = wide[:, h * H : (h + 1) * H] * m
        gsend[...] = half_gradient(other)
        to_partner = remote(gsend, grecv, s_g, r_g, partner)
        to_partner.start()
        own = half_gradient(c)
        to_partner.wait()
        total = (own + grecv[...]).astype(BF16)
        zsend[par] = total
        zrecv[par, z] = total
        sends = [
            remote(zsend.at[par], zrecv.at[par, z], s_z.at[i], r_z.at[par, z], (zp * 2 + c, col))
            for i, zp in enumerate(zpeers)
        ]
        for cp in sends:
            cp.start()

        @pl.when(k == 0)
        def _():
            for i, (dev, h) in enumerate(pdest):
                src = dev[0]
                remote(
                    pinit.at[pl.ds(h * 12, 12)], pgot.at[pl.ds(src * 12, 12)], s_pinit.at[i], r_pinit.at[src], dev
                ).wait_recv()
            for q in range(4):
                for i in range(nrow):
                    for b in range(3):
                        slab[q, i * 3 + b : i * 3 + b + 1, :] = pgot[i * 12 + q * 3 + b]

        for i, zp in enumerate(zpeers):
            remote(zsend.at[par], zrecv.at[par, zp], s_z.at[i], r_z.at[par, zp], (zp * 2 + c, col)).wait_recv()
        grad = zrecv[par, 0].astype(F32)
        for i in range(1, nz):
            grad = grad + zrecv[par, i].astype(F32)
        now = slab[0]
        new = jnp.minimum(slab[3], jnp.maximum(slab[2], now - STEP * (slab[1] - grad)))
        ext = (2.0 * new - now).astype(BF16)
        esend[...] = ext
        xg[0, 0:cb, :] = ext.astype(F32)
        to_partner2 = remote(esend, erecv, s_e, r_e, partner)
        to_partner2.start()
        slab[0] = new
        pstep = new - now
        pacc[pl.ds(k, 1), :] = jnp.sum(pstep * pstep, axis=0, keepdims=True)
        image = half_image(0, c)
        to_partner2.wait()
        xg[1, 0:cb, :] = erecv[...].astype(F32)
        image = (image + half_image(1, other)).astype(BF16)
        xsend[par] = image
        xrecv[par, col] = image
        for i, xp in enumerate(xpeers):
            remote(xsend.at[par], xrecv.at[par, col], s_x.at[i], r_x.at[par, col], (row, xp)).start()

        @pl.when(k == ITERS - 1)
        def _():
            prow[0] = to_lanes(pacc[...], 8)
            precv[col] = prow[0]
            plast[0] = slab[0]
            for i, xp in enumerate(xpeers):
                remote(prow, precv.at[pl.ds(col, 1)], s_p.at[i], r_p.at[col], (row, xp)).start()
            remote(plast.at[0], plast.at[1], s_l, r_l, partner).start()

        for i, zp in enumerate(zpeers):
            sends[i].wait_send()
        for i, xp in enumerate(xpeers):
            remote(xsend.at[par], xrecv.at[par, xp], s_x.at[i], r_x.at[par, xp], (row, xp)).wait()
        img = xrecv[par, 0].astype(F32)
        for i in range(1, ncol):
            img = img + xrecv[par, i].astype(F32)
        dnow = dslab[0]
        dnew = jnp.maximum(dnow + STEP * (dslab[1] - img), 0.0)
        dslab[0] = dnew
        dstep = dnew - dnow
        drow = jnp.sum(dstep * dstep, axis=0, keepdims=True)
        dacc[pl.ds(k, 1), :] = drow[:, :H] + drow[:, H:]
        return carry

    lax.fori_loop(0, ITERS, iteration, 0)

    for i, xp in enumerate(xpeers):
        remote(prow, precv.at[pl.ds(xp, 1)], s_p.at[i], r_p.at[xp], (row, xp)).wait()
    ptotal = precv[0]
    for i in range(1, ncol):
        ptotal = ptotal + precv[i]
    mine = to_lanes(dacc[...], 0) + ptotal
    frow[0] = mine
    frecv[row] = mine
    for i, dev in enumerate(group):
        remote(frow, frecv.at[pl.ds(row, 1)], s_f.at[i], r_f.at[row], dev).start()

    remote(plast.at[0], plast.at[1], s_l, r_l, partner).wait()
    for b in range(3):
        at = row * 3 + b
        pstage[pl.ds(b * 2 + c, 1), 0] = plast[0, pl.ds(at, 1), :]
        pstage[pl.ds(b * 2 + other, 1), 0] = plast[1, pl.ds(at, 1), :]
    for h in range(2):
        gath[h] = dslab[0, :, h * H : (h + 1) * H]
        dstage[h] = gath[h, pl.ds(col, 1), :]
    outs = [pltpu.make_async_copy(pstage.at[i, 0], primal_out.at[pl.ds(i * H, H)], sem_out.at[i]) for i in range(6)]
    outs += [pltpu.make_async_copy(dstage.at[h, 0], dual_out.at[pl.ds(h * H, H)], sem_out.at[6 + h]) for h in range(2)]
    for cp in outs:
        cp.start()
    for i in range(len(xgroup)):
        remote(dinit, dgot.at[pl.ds(0, 4)], s_dinit.at[i], r_dinit.at[0], xgroup[i]).wait_send()
    for i, (dev, h) in enumerate(pdest):
        remote(pinit.at[pl.ds(h * 12, 12)], pgot.at[pl.ds(0, 12)], s_pinit.at[i], r_pinit.at[0], dev).wait_send()
    for cp in outs:
        cp.wait()
    for i, dev in enumerate(group):
        remote(frow, frecv.at[pl.ds(dev[0], 1)], s_f.at[i], r_f.at[dev[0]], dev).wait()
    dsum = frecv[0]
    for i in range(1, nrow):
        dsum = dsum + frecv[i]
    psum = frecv[z * 2] + frecv[z * 2 + 1]
    dcol = jnp.sum(jnp.where(lane8 == sub8, dsum, 0.0), axis=1, keepdims=True)
    pcol = jnp.sum(jnp.where(lane8 == sub8 + 8, psum, 0.0), axis=1, keepdims=True)
    ptot = float(cb * W * ncol)
    dtot = float(rb * W * nrow)
    pair = lax.broadcasted_iota(jnp.int32, (8, 2), 1)
    norms_out[...] = jnp.sqrt(jnp.where(pair == 0, pcol * (1.0 / ptot), dcol * (1.0 / dtot)))


def per_device(nz, ny, nx, blocks, block_cols, objective, lower_bound, upper_bound, right_side, primal_init, dual_init):
    nrow, ncol = nz * 2, ny * nx
    rb, cb = ncol, 3 * nrow
    kg = rb * 2 * W
    hbm = pl.BlockSpec(memory_space=pl.ANY)
    V, D = pltpu.VMEM, pltpu.SemaphoreType.DMA
    nzp, nxp, ngr = nz - 1, ncol - 1, 2 * nz - 1
    return pl.pallas_call(
        functools.partial(kernel, nz, ny, nx),
        out_shape=(
            jax.ShapeDtypeStruct((3 * W,), F32),
            jax.ShapeDtypeStruct((W,), F32),
            jax.ShapeDtypeStruct((ITERS, 2), F32),
        ),
        in_specs=[pl.BlockSpec(memory_space=pltpu.SMEM)] + [hbm] * 7,
        out_specs=(hbm, hbm, pl.BlockSpec(memory_space=pltpu.VMEM)),
        scratch_shapes=[
            V((kg, W), BF16),
            V((2, rb * W, W), BF16),
            V((rb * 2, cb, H), BF16),
            V((cb, kg), BF16),
            V((rb, rb * W), BF16),
            V((4, cb, H), F32),
            V((2, rb, W), F32),
            V((rb, W), F32),
            V((24, 1, H), F32),
            V((nrow * 12, 1, H), F32),
            V((4, 1, H), F32),
            V((ncol * 4, 1, H), F32),
            V((cb, H), F32),
            V((cb, H), F32),
            V((2, cb, H), BF16),
            V((2, nz, cb, H), BF16),
            V((cb, H), BF16),
            V((cb, H), BF16),
            V((2, cb + 8, H), F32),
            V((2, rb, H), F32),
            V((2, rb, W), BF16),
            V((2, ncol, rb, W), BF16),
            V((8, H), F32),
            V((8, H), F32),
            V((1, 1, H), F32),
            V((ncol, 1, H), F32),
            V((1, 1, H), F32),
            V((nrow, 1, H), F32),
            V((2, cb, H), F32),
            V((6, 1, H), F32),
            V((2, 1, H), F32),
            D((CHUNKS,)),
            D((28,)),
            D((8,)),
            D((ngr,)), D((nrow,)), D((nxp,)), D((ncol,)),
            D(()), D(()), D(()), D(()),
            D((nzp,)), D((2, nz)), D((nxp,)), D((2, ncol)),
            D((nxp,)), D((ncol,)), D((ngr,)), D((nrow,)),
            D(()), D(()),
        ],
        compiler_params=pltpu.CompilerParams(
            collective_id=0, has_side_effects=True, vmem_limit_bytes=48 * 1024 * 1024
        ),
    )(
        block_cols, blocks.reshape(kg, W), objective, lower_bound, upper_bound, right_side, primal_init, dual_init
    )


def solution(mesh):
    nz = mesh.shape["row"] // 2
    nx = NX if mesh.shape["col"] == NX * NX else 2
    ny = mesh.shape["col"] // nx
    placed = (
        P("row", "col", None, None),
        P("row", "col"),
        P(("col", "row")),
        P(("col", "row")),
        P(("col", "row")),
        P(("row", "col")),
        P(("col", "row")),
        P(("row", "col")),
    )
    return jax.shard_map(
        functools.partial(per_device, nz, ny, nx),
        mesh=mesh,
        in_specs=placed,
        out_specs=(P(("col", "row")), P(("row", "col")), P()),
        check_vma=False,
    )
```

time: 405 us -> 145 us (0.36); the launches traced: 400 us -> 144 us
  blocking collectives: 244 us -> 0 us
  Pallas kernels: 0 us -> 135 us
  matrix products: 53.5 us -> 0 us
  waiting for transfers between devices: 49 us -> 0 us
  starting transfers between devices: 22.5 us -> 0 us
  other arithmetic: 20.5 us -> 0 us
    all_gather x10 -> x0, blocking collectives: 191 us -> none  [the longest x8 157 us: over_pieces(): tiles = lax.all_gather(array, axis)]
    pallas_call x0 -> x1, Pallas kernels: none -> 135 us  [per_device(): pl.pallas_call(functools.partial(kernel, nz, ny, nx), out_shape=(jax.Shap...]
    dot_general x32 -> x0, matrix products: 53.5 us -> none  [the longest x8 26.9 us: per_device(): jnp.einsum('rsab,rsb->ra', blocks, shaped, preferred_element_type=jnp.flo...]
    all_to_all x6 -> x0, waiting for transfers between devices: 49 us -> none  [from_everyone(): lax.all_to_all(jnp.broadcast_to(array[None], (count, *array.shape)), axis...]
    psum x4 -> x0, blocking collectives: 30.8 us -> none  [over_axes(): return functools.reduce(lax.psum, axes, array)]
    all_to_all x6 -> x0, starting transfers between devices: 22.5 us -> none  [from_everyone(): lax.all_to_all(jnp.broadcast_to(array[None], (count, *array.shape)), axis...]
    all_to_all x2 -> x0, blocking collectives: 21.9 us -> none  [from_everyone(): lax.all_to_all(jnp.broadcast_to(array[None], (count, *array.shape)), axis...]
    another operation x8 -> x0, other arithmetic: 10.6 us -> none  [per_device(): stacked = jnp.stack(history)]
  transfers between devices with their start and end apart: 6 -> 0, of which waited for: 6 -> 0; matrix products, arithmetic and copies ran while one was open for 0% -> 0% of each run, Pallas kernels for 0% -> 0%
where the time goes in v1:
time: 145 us; the launch traced here: 144 us
  Pallas kernels  135 us (93%)
  local copies, waits for them, and re-layouts  8.84 us (6%)
    pallas_call x1, Pallas kernels, per_device(): pl.pallas_call(functools.partial(kernel, nz, ny, nx), out_shape=(jax.Shap...  135 us
    unnamed x17, local copies, waits for them, and re-layouts  8.2 us

profile of v1, /device:TPU:1, one launch (start us, length us, event | category | flops | bytes accessed | tf_op | source)
XLA Modules:
  0.0 144.4 jit_solution(12388348268020246773)
XLA Ops:
  0.6 0.8 copy.11.cols
  1.4 0.0 copy-start
  1.4 2.2 %copy-done = bf16[16,2,256,256]{3,2,1,0:T(8,128)(2,1)S(1)} copy-done((bf16[16,2,256,256]{3,2,1,0:T(8,128)(2,1)S(1)}, bf16[16,2,256,256]{3,2,1,0:T(8,128)(2,1)}, u32[]{:S(2)}) %copy-start) | copy-done | bytes 4194328
  3.6 0.0 copy-start.1
  3.6 0.7 copy-done.1
  4.3 0.0 copy-start.2
  4.3 0.7 copy-done.2
  4.9 0.0 copy-start.3
  5.0 0.7 copy-done.3
  5.6 0.0 copy-start.4
  5.6 0.7 copy-done.4
  6.3 0.0 copy-start.5
  6.3 0.7 copy-done.5
  7.0 0.0 copy-start.6
  7.0 0.7 copy-done.6
  7.7 134.9 %shard_map.103 = (f32[768]{0:T(1024)S(1)}, f32[256]{0:T(256)S(1)}, f32[8,2]{1,0:T(8,128)S(1)}) custom-call(s32[16,2]{1,0:T(8,128)S(1)} %copy.11.cols, bf16[8192,256]{1,0:T(8,128)(2,1)S(1)} %bitcast.1, f32[768]{0:T(1024)S(1)} %copy-done.1, f32[768]{0:T(1024)S(1)} %copy-done.2, f32[768]{0:T(1024)S(1)} %copy-done.3, f32[256]{0:T(256)S(1)} %copy-done.5, ...), custom_call_target="tpu_custom_call" | custom-call | tf_op jit(solution)/shard_map/pallas_call | solution.py:314
  142.6 0.6 copy.12
  143.2 0.6 copy.15
  143.8 0.6 copy.16
Async XLA Ops:
  1.4 2.2 %copy-start = (bf16[16,2,256,256]{3,2,1,0:T(8,128)(2,1)S(1)}, bf16[16,2,256,256]{3,2,1,0:T(8,128)(2,1)}, u32[]{:S(2)}) copy-start(bf16[16,2,256,256]{3,2,1,0:T(8,128)(2,1)} %param.8) | copy-start | bytes 12582916
  3.6 0.7 copy-start.1
  4.3 0.7 copy-start.2
  4.9 0.7 copy-start.3
  5.6 0.7 copy-start.4
  6.3 0.7 copy-start.5
  7.0 0.7 copy-start.6
